TPU v7x, 512 devices: a whole 4x8x8 slice. The times are simulated.
512 devices in a mesh: row: 32 (over y_hi, x, core), col: 16 (over y_lo, z).
Axes of the slice: x: 4, y: 8 (y_hi: 4, y_lo: 2; y = y_hi * 2 + y_lo), z: 8, core: 2. Of those that a mesh axis runs over, the one named last changes fastest.
Arguments:
- amplitudes: bfloat16 [1024, 32768], P('row', 'col'), may hold values from -6 to 6
- integrals: bfloat16 [32768, 32768], P('col', 'row'), may hold values from -0.0390625 to 0.0390625
- tile_mask: int32 [256, 256], P('col', 'row'), may hold values 0 or 1
- driving: bfloat16 [1024, 32768], P('col', 'row'), may hold values from -6 to 6
- occupied_energy: float32 [1024], P('col'), may hold values from -1.5 to -0.5
- virtual_energy: float32 [32768], P('row'), may hold values from 0.5 to 2.5
Outputs:
- update: float32 [1024, 32768], P('col', 'row')
All inputs are finite; a program needn't handle non-finite values. No bound on the sum of `tile_mask` on one device may be relied on, other than what follows from the above.
Results may differ from a plain program's by a relative error of at most 0.0003.
Values may be sent and summed in bfloat16 or wider, within the bound.
A program may use at most 64 MiB of HBM per device.

v0:
```python
import jax
import jax.numpy as jnp
from jax import lax
from jax.sharding import PartitionSpec as P


def shards(amplitudes, integrals, tile_mask, driving, occupied_energy, virtual_energy):
    tiles_in = tile_mask.shape[0]
    tiles_out = tile_mask.shape[1]
    tile_size = integrals.shape[0] // tiles_in
    shaped = integrals.reshape(tiles_in, tile_size, tiles_out, tile_size)
    masked = (shaped * tile_mask.astype(jnp.bfloat16)[:, None, :, None]).reshape(integrals.shape)
    partial_sum = jnp.dot(
        lax.all_gather(amplitudes, "row", axis=0, tiled=True),
        masked,
        preferred_element_type=jnp.float32,
    )
    ladder = lax.psum_scatter(partial_sum, "col", scatter_dimension=0, tiled=True)
    denom = virtual_energy[None, :] - occupied_energy[:, None]
    return (driving.astype(jnp.float32) + ladder) / denom


def solution(mesh):
    in_specs = (
        P("row", "col"),
        P("col", "row"),
        P("col", "row"),
        P("col", "row"),
        P("col"),
        P("row"),
    )
    out_specs = P("col", "row")
    return jax.shard_map(shards, mesh=mesh, in_specs=in_specs, out_specs=out_specs, check_vma=False)
```

profile of v0, /device:TPU:2, one launch (start us, length us, event | category | flops | bytes accessed | tf_op | source)
XLA Modules:
  0.0 188.9 jit_solution(5905273928543527825)
XLA Ops:
  6.5 0.0 all-gather.2.cloned.1.call-start
  6.5 0.7 all-gather.2.cloned.1.call-update
  7.3 0.0 reduce-scatter.4.cloned.1.call-start
  7.3 0.7 convert_element_type.7
  8.0 0.1 copy.13
  8.1 72.6 %all-gather.2.cloned.1.call-done = bf16[1024,2048]{1,0:T(8,128)(2,1)} async-done(((bf16[32,2048]{1,0:T(8,128)(2,1)}), bf16[1024,2048]{1,0:T(8,128)(2,1)}) %all-gather.2.cloned.1.call-update) | async-done | bytes 4194320 | tf_op jit(solution)/shard_map/all_gather | solution.py:14
  80.7 0.0 copy-start.3
  80.7 0.6 mul.11
  81.3 1.6 copy-done.3
  82.9 8.8 %fusion.2 = f32[1024,1024]{0,1:T(8,128)} fusion(bf16[1024,2048]{1,0:T(8,128)(2,1)} %all-gather.2.cloned.1.call-done, bf16[2048,1024]{1,0:T(8,128)(2,1)S(1)} %copy-done.3, bf16[256,8,8,128]{3,2,1,0:T(8,128)(2,1)S(1)} %bitcast.11), kind=kOutput, calls=%fused_computation.3 | convolution fusion | flops 4297064448 | bytes 16777216 | tf_op jit(solution)/shard_map/dot_general | solution.py:13
  91.7 5.4 %copy.15 = f32[1024,1024]{1,0:T(8,128)} copy(f32[1024,1024]{0,1:T(8,128)} %fusion.2) | data formatting | bytes 8388608
  97.1 0.0 copy-start
  97.1 0.0 copy-start.1
  97.1 0.0 copy-start.2
  97.1 0.0 reduce-scatter.4.cloned.1.call-update
  97.1 83.2 %reduce-scatter.4.cloned.1.call-done = f32[64,1024]{1,0:T(8,128)} async-done(((f32[1024,1024]{1,0:T(8,128)}), f32[64,1024]{1,0:T(8,128)}) %reduce-scatter.4.cloned.1.call-update) | async-done | bytes 262160 | tf_op jit(solution)/shard_map/reduce_scatter | solution.py:18
  180.3 0.0 copy-done
  180.3 0.0 copy-done.1
  180.3 0.0 copy-done.2
  180.3 1.8 subtract_divide_fusion
Async XLA Ops:
  6.5 74.2 %all-gather.2.cloned.1.call-start = ((), (), s32[]{:S(2)}) async-start(), calls=%async_computation.1 | async-start | bytes 4325376 | tf_op jit(solution)/shard_map/all_gather | solution.py:14
  7.3 173.1 %reduce-scatter.4.cloned.1.call-start = ((), (), s32[]{:S(2)}) async-start(), calls=%async_computation.2 | async-start | bytes 4456448 | tf_op jit(solution)/shard_map/reduce_scatter | solution.py:18
  80.7 2.2 %copy-start.3 = (bf16[2048,1024]{1,0:T(8,128)(2,1)S(1)}, bf16[2048,1024]{1,0:T(8,128)(2,1)}, u32[]{:S(2)}) copy-start(bf16[2048,1024]{1,0:T(8,128)(2,1)} %param.7) | copy-start | bytes 12582916
  97.1 83.3 %copy-start = (bf16[64,1024]{1,0:T(8,128)(2,1)S(1)}, bf16[64,1024]{1,0:T(8,128)(2,1)}, u32[]{:S(2)}) copy-start(bf16[64,1024]{1,0:T(8,128)(2,1)} %param.9) | copy-start | bytes 393220
  97.1 83.3 %copy-start.1 = (f32[1024]{0:T(1024)S(1)}, f32[1024]{0:T(1024)}, u32[]{:S(2)}) copy-start(f32[1024]{0:T(1024)} %param.11) | copy-start | bytes 12292
  97.1 83.3 %copy-start.2 = (f32[64]{0:T(128)S(1)}, f32[64]{0:T(128)}, u32[]{:S(2)}) copy-start(f32[64]{0:T(128)} %param.10) | copy-start | bytes 772
Sparse Core Ops, SparseCore 0:
  10.5 70.1 all-gather.1
  97.2 83.0 reduce-scatter.3
where the time goes:
time: 189 us
  waiting for transfers between devices  157 us (83%)
  between operations  13.4 us (7%)
  matrix products  8.82 us (5%)
  local copies, waits for them, and re-layouts  7.65 us (4%)
  other arithmetic  2.45 us (1%)
    reduce_scatter x1, waiting for transfers between devices, shards(): lax.psum_scatter(partial_sum, 'col', scatter_dimension=0, tiled=True)  83.2 us
    all_gather x1, waiting for transfers between devices, shards(): lax.all_gather(amplitudes, 'row', axis=0, tiled=True)  72.6 us
    dot_general x1, matrix products, shards(): jnp.dot(lax.all_gather(amplitudes, 'row', axis=0, tiled=True), masked, pr...  8.82 us
    unnamed x9, local copies, waits for them, and re-layouts  6.95 us
  transfers between devices with their start and end apart: 2, of which 2 were waited for; matrix products, arithmetic and copies ran while one was open for 0% of the time, Pallas kernels for 0%

commit v1 on v0

v1 whole, which is shorter than its diff:
```python
import functools

import jax
import jax.numpy as jnp
from jax import lax
from jax.experimental import pallas as pl
from jax.experimental.pallas import tpu as pltpu
from jax.sharding import PartitionSpec as P

MESH = pl.DeviceIdType.MESH
TOP = 32767.0
TINY = 1e-30

UNITS = (
    (0, 0),
    (1, 0), (-1, 0),
    (2, 0), (0, 1), (0, -1),
    (1, 1), (1, -1), (-1, 1), (-1, -1), (0, 2),
    (2, 1), (2, -1), (1, 2), (-1, 2),
    (2, 2),
)
SLOT = {unit: slot for slot, unit in enumerate(UNITS)}
GROUPS = ((0, 1), (1, 3), (3, 6), (6, 11), (11, 15), (15, 16))
GROUP_AT = (3.5, 6.5, 10.5, 15.5, 19.0, 21.5)
HOP = 4.0
DYS = (0, 1, -1, 2)


def kernel(a_ref, m_hbm, mask_ref, out_ref, held, m_ref, part, q_out, s_out, q_in, s_in, total, yq_out, ys_out, yq_in, ys_in,
           m_sem, own_sem, ag_send, ag_recv, z_send, z_recv, zs_send, zs_recv, y_sem):
    row, col = lax.axis_index("row"), lax.axis_index("col")
    core = lax.rem(row, 2)
    x = lax.rem(row // 2, 4)
    y = row // 8
    z = lax.rem(col, 8)
    y_lo = col // 8
    depth = a_ref.shape[0]
    half = depth // 2
    rows = 2 * depth

    def at_xy(dx, dy):
        return ((lax.rem(y + dy + 4, 4) * 4 + lax.rem(x + dx + 4, 4)) * 2 + core, col)

    def at_z(dz):
        return (row, y_lo * 8 + lax.rem(z + dz + 8, 8))

    sibling = ((y * 4 + x) * 2 + (1 - core), col)
    mate = (row, (1 - y_lo) * 8 + z)
    partners = (at_xy(1, 0), at_xy(-1, 0), at_xy(0, 1), at_xy(0, -1), sibling, at_z(1), at_z(-1), mate)

    chunks = m_sem.shape[0]
    step = m_ref.shape[0] // chunks
    loads = [
        pltpu.make_async_copy(m_hbm.at[pl.ds(i * step, step)], m_ref.at[pl.ds(i * step, step)], m_sem.at[i])
        for i in range(chunks)
    ]
    for load in loads:
        load.start()
    own = pltpu.make_async_copy(a_ref, held.at[pl.ds(core * depth, depth)], own_sem)
    own.start()

    barrier = pltpu.get_barrier_semaphore()
    for partner in partners:
        pl.semaphore_signal(barrier, inc=1, device_id=partner, device_id_type=MESH)
    pl.semaphore_wait(barrier, len(partners))

    kinds = {}

    def piece(unit, part_of):
        start = SLOT[unit] * rows + core * depth
        if part_of is None:
            return held.at[pl.ds(start, depth)]
        return held.at[pl.ds(start + part_of * half, half)]

    def message(kind, source, target_unit, part_of, device):
        index = kinds.setdefault(kind, len(kinds))
        return pltpu.make_async_remote_copy(
            src_ref=source, dst_ref=piece(target_unit, part_of), send_sem=ag_send.at[index], recv_sem=ag_recv.at[index],
            device_id=device, device_id_type=MESH)

    sent = {}

    def send(kind, source, target_unit, part_of, device):
        copy = message(kind, source, target_unit, part_of, device)
        copy.start()
        sent[kind] = copy

    def own_half(h):
        return a_ref.at[pl.ds(h * half, half)]

    def source(unit, h):
        if unit == (0, 0):
            return a_ref if h is None else own_half(h)
        return piece(unit, h)

    def wrap(d):
        return 2 if d == -2 else d

    def got(kind):
        sent[kind].wait_recv()

    def to_sibling(unit, h=None):
        send(("s", unit, h), source(unit, h), unit, h, sibling)

    def x_first(dy, h):
        order = (1, -1) if h == 0 else (-1, 1)
        for dx in order:
            send(("x1", dx, dy, h), source((0, dy), h), (-dx, dy), h, at_xy(dx, 0))

    def x_second(dx, dy):
        h = 0 if dx == 1 else 1
        send(("x2", dx, dy), piece((-dx, dy), h), (2, dy), h, at_xy(dx, 0))

    def y_second(dy):
        h = 0 if dy == 1 else 1
        send(("y2", dy), piece((0, -dy), h), (0, 2), h, at_xy(0, dy))

    def act_y1(dy, h):
        def run():
            got(("y1", dy, h))
            first = 0 if dy == 1 else 1
            if h == first:
                y_second(dy)
            x_first(-dy, h)
            if h != first:
                to_sibling((0, -dy))
        return run

    def act_y2(dy):
        def run():
            got(("y2", dy))
            h = 0 if dy == 1 else 1
            x_first(2, h)
            to_sibling((0, 2), h)
        return run

    def act_x1(dx, dy, h):
        def run():
            got(("x1", dx, dy, h))
            if h == (0 if dx == 1 else 1):
                x_second(dx, dy)
            to_sibling((-dx, dy), h)
        return run

    def act_x2(dx, dy):
        def run():
            got(("x2", dx, dy))
            to_sibling((2, dy), 0 if dx == 1 else 1)
        return run

    for h in (0, 1):
        for dy in (1, -1):
            ph = h if dy == 1 else 1 - h
            send(("y1", dy, ph), own_half(ph), (0, -dy), ph, at_xy(0, dy))
        for dx in (1, -1):
            ph = h if dx == 1 else 1 - h
            send(("x1", dx, 0, ph), own_half(ph), (-dx, 0), ph, at_xy(dx, 0))
        if h == 0:
            to_sibling((0, 0))

    tiles = 128
    for i in range(chunks):
        loads[i].wait()

        @pl.loop(0, step // tiles)
        def _(t, i=i):
            for j in range(m_ref.shape[1] // tiles):
                filled = mask_ref[i * (step // tiles) + t, j].astype(jnp.float32)
                here = (pl.ds(pl.multiple_of(i * step + t * tiles, tiles), tiles), pl.ds(j * tiles, tiles))
                m_ref[here] = m_ref[here] * filled.astype(jnp.bfloat16)

    own.wait()

    wide = 256

    def act_mm(lo, hi):
        def run():
            for slot in range(lo, hi):
                for kind in sibling_kinds[slot]:
                    got(kind)
            span = pl.ds(lo * rows, (hi - lo) * rows)

            @pl.loop(0, m_ref.shape[1] // wide)
            def _(n):
                across = pl.ds(pl.multiple_of(n * wide, wide), wide)
                part[span, across] = jnp.dot(held[span, :], m_ref[:, across], preferred_element_type=jnp.float32)
        return run

    lanes = 256

    def encode(value, q_ref, s_ref, t):
        top = jnp.max(jnp.abs(value), axis=0, keepdims=True)
        top = jnp.maximum(top, TINY)
        q_ref[:, pl.ds(pl.multiple_of(t * lanes, lanes), lanes)] = jnp.round(value * (TOP / top)).astype(jnp.int16)
        s_ref[pl.ds(t, 1), :] = top * (1.0 / TOP)

    def decode(q_ref, s_ref, t):
        return q_ref[:, pl.ds(pl.multiple_of(t * lanes, lanes), lanes)].astype(jnp.float32) * s_ref[pl.ds(t, 1), :]

    def over_lanes(body):
        pl.loop(0, part.shape[1] // lanes)(body)

    def where_is(slot):
        dx, dy = UNITS[slot]
        ux, uy = lax.rem(x + dx + 4, 4), lax.rem(y + dy + 4, 4)
        lo = uy // 2
        d = lax.rem(z - (lax.rem(uy, 2) * 4 + ux) + 8, 8)
        down = (d < 4) | ((d == 4) & (lo == 0))
        p = jnp.where(d <= 4, d, 8 - d)
        first = (p == 4) | ((p == 3) & (down != (lo == 0)))
        return d, p, down, first, lo

    def z_copies(slot, way):
        device = at_z(-1 if way == 0 else 1)
        return (
            pltpu.make_async_remote_copy(
                src_ref=q_out.at[slot], dst_ref=q_in.at[slot, way], send_sem=z_send.at[slot], recv_sem=z_recv.at[slot, way],
                device_id=device, device_id_type=MESH),
            pltpu.make_async_remote_copy(
                src_ref=s_out.at[slot], dst_ref=s_in.at[slot, way], send_sem=zs_send.at[slot], recv_sem=zs_recv.at[slot, way],
                device_id=device, device_id_type=MESH),
        )

    def z_start(slot, down):
        for way in (0, 1):
            @pl.when(down if way == 0 else jnp.logical_not(down))
            def _():
                for copy in z_copies(slot, way):
                    copy.start()

    def own_part(slot, t):
        return part[pl.ds(slot * rows, rows), pl.ds(pl.multiple_of(t * lanes, lanes), lanes)]

    def act_start(slot):
        def run():
            d, p, down, first, lo = where_is(slot)

            @pl.when(first)
            def _():
                over_lanes(lambda t: encode(own_part(slot, t), q_out.at[slot], s_out.at[slot], t))
                z_start(slot, down)
        return run

    def act_hop(slot, at):
        def run():
            d, p, down, first, lo = where_is(slot)
            for way in (0, 1):
                @pl.when((p == at) & jnp.logical_not(first) & (down if way == 0 else jnp.logical_not(down)))
                def _():
                    for copy in z_copies(slot, way):
                        copy.wait_recv()
                    over_lanes(lambda t: encode(
                        own_part(slot, t) + decode(q_in.at[slot, way], s_in.at[slot, way], t),
                        q_out.at[slot], s_out.at[slot], t))
                    for copy in z_copies(slot, way):
                        copy.start()
        return run

    y_copies = (
        pltpu.make_async_remote_copy(src_ref=yq_out, dst_ref=yq_in, send_sem=y_sem.at[0], recv_sem=y_sem.at[1],
                                     device_id=mate, device_id_type=MESH),
        pltpu.make_async_remote_copy(src_ref=ys_out, dst_ref=ys_in, send_sem=y_sem.at[2], recv_sem=y_sem.at[3],
                                     device_id=mate, device_id_type=MESH),
    )

    def act_end(slot):
        def run():
            d, p, down, first, lo = where_is(slot)

            @pl.when(d == 0)
            def _():
                for way in (0, 1):
                    for copy in z_copies(slot, way):
                        copy.wait_recv()

                def summed(t):
                    return (own_part(slot, t) + decode(q_in.at[slot, 0], s_in.at[slot, 0], t)
                            + decode(q_in.at[slot, 1], s_in.at[slot, 1], t))

                @pl.when(lo != y_lo)
                def _():
                    over_lanes(lambda t: encode(summed(t), yq_out, ys_out, t))
                    for copy in y_copies:
                        copy.start()

                @pl.when(lo == y_lo)
                def _():
                    def keep(t):
                        total[:, pl.ds(pl.multiple_of(t * lanes, lanes), lanes)] = summed(t)
                    over_lanes(keep)
        return run

    acts = []
    for dx in (1, -1):
        f = 0 if dx == 1 else 1
        acts.append((3.0, act_x1(dx, 0, f)))
        acts.append((4.5, act_x1(dx, 0, 1 - f)))
        acts.append((6.3, act_x2(dx, 0)))
        for dy in (1, -1):
            acts.append((9.0, act_x1(dx, dy, f)))
            acts.append((12.0, act_x1(dx, dy, 1 - f)))
            acts.append((13.5, act_x2(dx, dy)))
        acts.append((14.8, act_x1(dx, 2, f)))
        acts.append((16.0, act_x1(dx, 2, 1 - f)))
        acts.append((18.5, act_x2(dx, 2)))
    for dy in (1, -1):
        f = 0 if dy == 1 else 1
        acts.append((5.3, act_y1(dy, f)))
        acts.append((8.1, act_y1(dy, 1 - f)))
        acts.append((11.3, act_y2(dy)))
    for (lo, hi), at in zip(GROUPS, GROUP_AT):
        acts.append((at, act_mm(lo, hi)))
        for slot in range(lo, hi):
            acts.append((at + 0.01, act_start(slot)))
            for k in (3, 2, 1):
                acts.append((at + 1.0 + HOP * (4 - k), act_hop(slot, k)))
            acts.append((at + 1.0 + HOP * 4, act_end(slot)))
    acts.sort(key=lambda act: act[0])

    sibling_kinds = []
    for unit in UNITS:
        dx, dy = unit
        whole = dx == 0 and dy != 2
        sibling_kinds.append([("s", unit, None)] if whole else [("s", unit, 0), ("s", unit, 1)])

    for _, run in acts:
        run()

    for copy in y_copies:
        copy.wait_recv()

    def finish(t):
        across = pl.ds(pl.multiple_of(t * lanes, lanes), lanes)
        out_ref[:, across] = total[:, across] + decode(yq_in, ys_in, t)
    over_lanes(finish)

    for copy in sent.values():
        copy.wait_send()
    for slot in range(len(UNITS)):
        d = where_is(slot)[0]

        @pl.when(d != 0)
        def _():
            for copy in z_copies(slot, 0):
                copy.wait_send()
    for copy in y_copies:
        copy.wait_send()


def gathered_product(amplitudes, integrals, tile_mask):
    depth, inner = amplitudes.shape
    width = integrals.shape[1]
    rows = 2 * depth
    n = len(UNITS)
    groups = width // 256
    vmem = pltpu.VMEM
    dma = pltpu.SemaphoreType.DMA
    messages = 64
    return pl.pallas_call(
        kernel,
        out_shape=jax.ShapeDtypeStruct((rows, width), jnp.float32),
        in_specs=[
            pl.BlockSpec(memory_space=pltpu.VMEM),
            pl.BlockSpec(memory_space=pl.ANY),
            pl.BlockSpec(memory_space=pltpu.SMEM),
        ],
        out_specs=pl.BlockSpec(memory_space=pltpu.VMEM),
        scratch_shapes=[
            vmem((n * rows, inner), jnp.bfloat16),
            vmem((inner, width), jnp.bfloat16),
            vmem((n * rows, width), jnp.float32),
            vmem((n, rows, width), jnp.int16),
            vmem((n, groups, 256), jnp.float32),
            vmem((n, 2, rows, width), jnp.int16),
            vmem((n, 2, groups, 256), jnp.float32),
            vmem((rows, width), jnp.float32),
            vmem((rows, width), jnp.int16),
            vmem((groups, 256), jnp.float32),
            vmem((rows, width), jnp.int16),
            vmem((groups, 256), jnp.float32),
            dma((4,)),
            dma,
            dma((messages,)),
            dma((messages,)),
            dma((n,)),
            dma((n, 2)),
            dma((n,)),
            dma((n, 2)),
            dma((4,)),
        ],
        compiler_params=pltpu.CompilerParams(
            collective_id=0, has_side_effects=True, vmem_limit_bytes=48 * 1024 * 1024),
        name="ladder",
    )(amplitudes, integrals, tile_mask)


def shards(amplitudes, integrals, tile_mask, driving, occupied_energy, virtual_energy):
    ladder = gathered_product(amplitudes, integrals, tile_mask)
    denom = virtual_energy[None, :] - occupied_energy[:, None]
    return (driving.astype(jnp.float32) + ladder) / denom


def solution(mesh):
    in_specs = (
        P("row", "col"),
        P("col", "row"),
        P("col", "row"),
        P("col", "row"),
        P("col"),
        P("row"),
    )
    out_specs = P("col", "row")
    return jax.shard_map(shards, mesh=mesh, in_specs=in_specs, out_specs=out_specs, check_vma=False)
```

time: 189 us -> 86.9 us (0.46)
  the two profiles are of different devices: /device:TPU:2 before, /device:TPU:202 now
where the time goes in v1:
time: 86.9 us; the launch traced here: 86.7 us
  Pallas kernels  81.9 us (94%)
  local copies, waits for them, and re-layouts  3.89 us (4%)
    pallas_call x1, Pallas kernels, gathered_product(): pl.pallas_call(kernel, out_shape=jax.ShapeDtypeStruct((rows, width), jnp....  81.9 us
    unnamed x11, local copies, waits for them, and re-layouts  3.89 us

profile of v1, /device:TPU:202, one launch (start us, length us, event | category | flops | bytes accessed | tf_op | source)
XLA Modules:
  0.0 86.7 jit_solution(11948173638184224394)
XLA Ops:
  0.0 0.0 copy-start.3
  0.0 0.0 copy-start.4
  0.0 0.8 copy.7.mask_ref
  0.8 0.0 copy-start
  0.8 2.2 %copy-done = bf16[2048,1024]{1,0:T(8,128)(2,1)S(1)} copy-done((bf16[2048,1024]{1,0:T(8,128)(2,1)S(1)}, bf16[2048,1024]{1,0:T(8,128)(2,1)}, u32[]{:S(2)}) %copy-start) | copy-done | bytes 4194328
  3.0 0.0 copy-start.1
  3.0 0.9 %copy-done.1 = bf16[32,2048]{1,0:T(8,128)(2,1)S(1)} copy-done((bf16[32,2048]{1,0:T(8,128)(2,1)S(1)}, bf16[32,2048]{1,0:T(8,128)(2,1)}, u32[]{:S(2)}) %copy-start.1) | copy-done | bytes 131096
  3.9 0.0 copy-start.2
  3.9 81.9 %ladder.1 = f32[64,1024]{1,0:T(8,128)S(1)} custom-call(bf16[32,2048]{1,0:T(8,128)(2,1)S(1)} %copy-done.1, bf16[2048,1024]{1,0:T(8,128)(2,1)S(1)} %copy-done, s32[16,8]{1,0:T(8,128)S(1)} %copy.7.mask_ref), custom_call_target="tpu_custom_call" | custom-call | tf_op jit(solution)/shard_map/ladder/pallas_call | solution.py:359
  85.8 0.0 copy-done.3
  85.8 0.0 copy-done.4
  85.9 0.0 copy-done.2
  85.9 0.8 subtract_divide_fusion
Async XLA Ops:
  0.0 85.8 %copy-start.3 = (f32[1024]{0:T(1024)S(1)}, f32[1024]{0:T(1024)}, u32[]{:S(2)}) copy-start(f32[1024]{0:T(1024)} %param.11) | copy-start | bytes 12292
  0.0 85.8 %copy-start.4 = (f32[64]{0:T(128)S(1)}, f32[64]{0:T(128)}, u32[]{:S(2)}) copy-start(f32[64]{0:T(128)} %param.10) | copy-start | bytes 772
  0.8 2.2 %copy-start = (bf16[2048,1024]{1,0:T(8,128)(2,1)S(1)}, bf16[2048,1024]{1,0:T(8,128)(2,1)}, u32[]{:S(2)}) copy-start(bf16[2048,1024]{1,0:T(8,128)(2,1)} %m_hbm.1) | copy-start | bytes 12582916
  3.0 0.9 %copy-start.1 = (bf16[32,2048]{1,0:T(8,128)(2,1)S(1)}, bf16[32,2048]{1,0:T(8,128)(2,1)}, u32[]{:S(2)}) copy-start(bf16[32,2048]{1,0:T(8,128)(2,1)} %a_ref.1) | copy-start | bytes 393220
  3.9 82.0 %copy-start.2 = (bf16[64,1024]{1,0:T(8,128)(2,1)S(1)}, bf16[64,1024]{1,0:T(8,128)(2,1)}, u32[]{:S(2)}) copy-start(bf16[64,1024]{1,0:T(8,128)(2,1)} %param.9) | copy-start | bytes 393220

commit v2 on v1

--- a/solution.py
+++ b/solution.py
@@ -22,7 +22,7 @@
 SLOT = {unit: slot for slot, unit in enumerate(UNITS)}
 GROUPS = ((0, 1), (1, 3), (3, 6), (6, 11), (11, 15), (15, 16))
 GROUP_AT = (3.5, 6.5, 10.5, 15.5, 19.0, 21.5)
-HOP = 4.0
+HOP = 3.5
 DYS = (0, 1, -1, 2)
 
 
@@ -191,11 +191,11 @@
     def encode(value, q_ref, s_ref, t):
         top = jnp.max(jnp.abs(value), axis=0, keepdims=True)
         top = jnp.maximum(top, TINY)
-        q_ref[:, pl.ds(pl.multiple_of(t * lanes, lanes), lanes)] = jnp.round(value * (TOP / top)).astype(jnp.int16)
-        s_ref[pl.ds(t, 1), :] = top * (1.0 / TOP)
+        q_ref[t] = jnp.round(value * (TOP / top)).astype(jnp.int16)
+        s_ref[t] = top * (1.0 / TOP)
 
     def decode(q_ref, s_ref, t):
-        return q_ref[:, pl.ds(pl.multiple_of(t * lanes, lanes), lanes)].astype(jnp.float32) * s_ref[pl.ds(t, 1), :]
+        return q_ref[t].astype(jnp.float32) * s_ref[t]
 
     def over_lanes(body):
         pl.loop(0, part.shape[1] // lanes)(body)
@@ -210,35 +210,33 @@
         first = (p == 4) | ((p == 3) & (down != (lo == 0)))
         return d, p, down, first, lo
 
-    def z_copies(slot, way):
+    def z_copies(slot, way, t):
         device = at_z(-1 if way == 0 else 1)
         return (
             pltpu.make_async_remote_copy(
-                src_ref=q_out.at[slot], dst_ref=q_in.at[slot, way], send_sem=z_send.at[slot], recv_sem=z_recv.at[slot, way],
+                src_ref=q_out.at[slot, t], dst_ref=q_in.at[slot, way, t],
+                send_sem=z_send.at[slot, t], recv_sem=z_recv.at[slot, way, t],
                 device_id=device, device_id_type=MESH),
             pltpu.make_async_remote_copy(
-                src_ref=s_out.at[slot], dst_ref=s_in.at[slot, way], send_sem=zs_send.at[slot], recv_sem=zs_recv.at[slot, way],
+                src_ref=s_out.at[slot, t], dst_ref=s_in.at[slot, way, t],
+                send_sem=zs_send.at[slot, t], recv_sem=zs_recv.at[slot, way, t],
                 device_id=device, device_id_type=MESH),
         )
 
-    def z_start(slot, down):
-        for way in (0, 1):
-            @pl.when(down if way == 0 else jnp.logical_not(down))
-            def _():
-                for copy in z_copies(slot, way):
-                    copy.start()
-
     def own_part(slot, t):
         return part[pl.ds(slot * rows, rows), pl.ds(pl.multiple_of(t * lanes, lanes), lanes)]
 
     def act_start(slot):
         def run():
             d, p, down, first, lo = where_is(slot)
-
-            @pl.when(first)
-            def _():
-                over_lanes(lambda t: encode(own_part(slot, t), q_out.at[slot], s_out.at[slot], t))
-                z_start(slot, down)
+            for way in (0, 1):
+                @pl.when(first & (down if way == 0 else jnp.logical_not(down)))
+                def _():
+                    def go(t):
+                        encode(own_part(slot, t), q_out.at[slot], s_out.at[slot], t)
+                        for copy in z_copies(slot, way, t):
+                            copy.start()
+                    over_lanes(go)
         return run
 
     def act_hop(slot, at):
@@ -247,47 +245,50 @@
             for way in (0, 1):
                 @pl.when((p == at) & jnp.logical_not(first) & (down if way == 0 else jnp.logical_not(down)))
                 def _():
-                    for copy in z_copies(slot, way):
+                    def go(t):
+                        for copy in z_copies(slot, way, t):
+                            copy.wait_recv()
+                        encode(own_part(slot, t) + decode(q_in.at[slot, way], s_in.at[slot, way], t),
+                               q_out.at[slot], s_out.at[slot], t)
+                        for copy in z_copies(slot, way, t):
+                            copy.start()
+                    over_lanes(go)
+        return run
+
+    def y_copies(t):
+        return (
+            pltpu.make_async_remote_copy(
+                src_ref=yq_out.at[t], dst_ref=yq_in.at[t], send_sem=y_sem.at[0, t], recv_sem=y_sem.at[1, t],
+                device_id=mate, device_id_type=MESH),
+            pltpu.make_async_remote_copy(
+                src_ref=ys_out.at[t], dst_ref=ys_in.at[t], send_sem=y_sem.at[2, t], recv_sem=y_sem.at[3, t],
+                device_id=mate, device_id_type=MESH),
+        )
+
+    def act_end(slot):
+        def run():
+            d, p, down, first, lo = where_is(slot)
+
+            def summed(t):
+                for way in (0, 1):
+                    for copy in z_copies(slot, way, t):
                         copy.wait_recv()
-                    over_lanes(lambda t: encode(
-                        own_part(slot, t) + decode(q_in.at[slot, way], s_in.at[slot, way], t),
-                        q_out.at[slot], s_out.at[slot], t))
-                    for copy in z_copies(slot, way):
+                return (own_part(slot, t) + decode(q_in.at[slot, 0], s_in.at[slot, 0], t)
+                        + decode(q_in.at[slot, 1], s_in.at[slot, 1], t))
+
+            @pl.when((d == 0) & (lo != y_lo))
+            def _():
+                def go(t):
+                    encode(summed(t), yq_out, ys_out, t)
+                    for copy in y_copies(t):
                         copy.start()
-        return run
-
-    y_copies = (
-        pltpu.make_async_remote_copy(src_ref=yq_out, dst_ref=yq_in, send_sem=y_sem.at[0], recv_sem=y_sem.at[1],
-                                     device_id=mate, device_id_type=MESH),
-        pltpu.make_async_remote_copy(src_ref=ys_out, dst_ref=ys_in, send_sem=y_sem.at[2], recv_sem=y_sem.at[3],
-                                     device_id=mate, device_id_type=MESH),
-    )
-
-    def act_end(slot):
-        def run():
-            d, p, down, first, lo = where_is(slot)
-
-            @pl.when(d == 0)
+                over_lanes(go)
+
+            @pl.when((d == 0) & (lo == y_lo))
             def _():
-                for way in (0, 1):
-                    for copy in z_copies(slot, way):
-                        copy.wait_recv()
-
-                def summed(t):
-                    return (own_part(slot, t) + decode(q_in.at[slot, 0], s_in.at[slot, 0], t)
-                            + decode(q_in.at[slot, 1], s_in.at[slot, 1], t))
-
-                @pl.when(lo != y_lo)
-                def _():
-                    over_lanes(lambda t: encode(summed(t), yq_out, ys_out, t))
-                    for copy in y_copies:
-                        copy.start()
-
-                @pl.when(lo == y_lo)
-                def _():
-                    def keep(t):
-                        total[:, pl.ds(pl.multiple_of(t * lanes, lanes), lanes)] = summed(t)
-                    over_lanes(keep)
+                def keep(t):
+                    total[:, pl.ds(pl.multiple_of(t * lanes, lanes), lanes)] = summed(t)
+                over_lanes(keep)
         return run
 
     acts = []
@@ -326,10 +327,9 @@
     for _, run in acts:
         run()
 
-    for copy in y_copies:
-        copy.wait_recv()
-
     def finish(t):
+        for copy in y_copies(t):
+            copy.wait_recv()
         across = pl.ds(pl.multiple_of(t * lanes, lanes), lanes)
         out_ref[:, across] = total[:, across] + decode(yq_in, ys_in, t)
     over_lanes(finish)
@@ -341,10 +341,15 @@
 
         @pl.when(d != 0)
         def _():
-            for copy in z_copies(slot, 0):
-                copy.wait_send()
-    for copy in y_copies:
-        copy.wait_send()
+            def gone(t):
+                for copy in z_copies(slot, 0, t):
+                    copy.wait_send()
+            over_lanes(gone)
+
+    def handed(t):
+        for copy in y_copies(t):
+            copy.wait_send()
+    over_lanes(handed)
 
 
 def gathered_product(amplitudes, integrals, tile_mask):
@@ -360,8 +365,8 @@
         kernel,
         out_shape=jax.ShapeDtypeStruct((rows, width), jnp.float32),
         in_specs=[
-            pl.BlockSpec(memory_space=pltpu.VMEM),
-            pl.BlockSpec(memory_space=pl.ANY),
+            pl.BlockSpec(memory_space=pltpu.HBM),
+            pl.BlockSpec(memory_space=pltpu.HBM),
             pl.BlockSpec(memory_space=pltpu.SMEM),
         ],
         out_specs=pl.BlockSpec(memory_space=pltpu.VMEM),
@@ -369,27 +374,27 @@
             vmem((n * rows, inner), jnp.bfloat16),
             vmem((inner, width), jnp.bfloat16),
             vmem((n * rows, width), jnp.float32),
-            vmem((n, rows, width), jnp.int16),
-            vmem((n, groups, 256), jnp.float32),
-            vmem((n, 2, rows, width), jnp.int16),
-            vmem((n, 2, groups, 256), jnp.float32),
+            vmem((n, groups, rows, 256), jnp.int16),
+            vmem((n, groups, 1, 256), jnp.float32),
+            vmem((n, 2, groups, rows, 256), jnp.int16),
+            vmem((n, 2, groups, 1, 256), jnp.float32),
             vmem((rows, width), jnp.float32),
-            vmem((rows, width), jnp.int16),
-            vmem((groups, 256), jnp.float32),
-            vmem((rows, width), jnp.int16),
-            vmem((groups, 256), jnp.float32),
+            vmem((groups, rows, 256), jnp.int16),
+            vmem((groups, 1, 256), jnp.float32),
+            vmem((groups, rows, 256), jnp.int16),
+            vmem((groups, 1, 256), jnp.float32),
             dma((4,)),
             dma,
             dma((messages,)),
             dma((messages,)),
-            dma((n,)),
-            dma((n, 2)),
-            dma((n,)),
-            dma((n, 2)),
-            dma((4,)),
+            dma((n, groups)),
+            dma((n, 2, groups)),
+            dma((n, groups)),
+            dma((n, 2, groups)),
+            dma((4, groups)),
         ],
         compiler_params=pltpu.CompilerParams(
-            collective_id=0, has_side_effects=True, vmem_limit_bytes=48 * 1024 * 1024),
+            collective_id=0, has_side_effects=True, vmem_limit_bytes=63 * 1024 * 1024),
         name="ladder",
     )(amplitudes, integrals, tile_mask)
 

time: 86.9 us -> 83.3 us (0.959)
  the two profiles are of different devices: /device:TPU:202 before, /device:TPU:60 now
where the time goes in v2:
time: 83.3 us; the launch traced here: 83.1 us
  Pallas kernels  79.9 us (96%)
  other arithmetic  1.76 us (2%)
  local copies, waits for them, and re-layouts  1.4 us (2%)
    pallas_call x1, Pallas kernels, gathered_product(): pl.pallas_call(kernel, out_shape=jax.ShapeDtypeStruct((rows, width), jnp....  79.9 us
    div x1, other arithmetic, shards(): return (driving.astype(jnp.float32) + ladder) / denom  1.76 us

profile of v2, /device:TPU:60, one launch (start us, length us, event | category | flops | bytes accessed | tf_op | source)
XLA Modules:
  0.0 83.1 jit_solution(15614686676091162077)
XLA Ops:
  0.0 0.0 copy-start.1
  0.0 0.0 copy-start.2
  0.0 0.0 copy-start
  0.0 1.4 %copy.7.mask_ref = s32[16,8]{1,0:T(8,128)} copy(s32[16,8]{0,1:T(8,128)} %param.8) | data formatting | bytes 1024 | tf_op args[2]
  1.4 79.9 %ladder.1 = f32[64,1024]{1,0:T(8,128)} custom-call(bf16[32,2048]{1,0:T(8,128)(2,1)} %a_ref.1, bf16[2048,1024]{1,0:T(8,128)(2,1)} %m_hbm.1, s32[16,8]{1,0:T(8,128)} %copy.7.mask_ref), custom_call_target="tpu_custom_call" | custom-call | tf_op jit(solution)/shard_map/ladder/pallas_call | solution.py:364
  81.3 0.0 copy-done.1
  81.3 0.0 copy-done.2
  81.3 0.0 copy-done
  81.3 1.8 %subtract_divide_fusion = f32[64,1024]{1,0:T(8,128)} fusion(f32[64,1024]{1,0:T(8,128)} %ladder.1, bf16[64,1024]{1,0:T(8,128)(2,1)S(1)} %copy-done, f32[64]{0:T(128)S(1)} %copy-done.2, f32[1024]{0:T(1024)S(1)} %copy-done.1), kind=kLoop, calls=%fused_computation | loop fusion | flops 262144 | bytes 659712 | tf_op jit(solution)/shard_map/div | solution.py:405
Async XLA Ops:
  0.0 81.3 %copy-start.1 = (f32[1024]{0:T(1024)S(1)}, f32[1024]{0:T(1024)}, u32[]{:S(2)}) copy-start(f32[1024]{0:T(1024)} %param.11) | copy-start | bytes 12292
  0.0 81.3 %copy-start.2 = (f32[64]{0:T(128)S(1)}, f32[64]{0:T(128)}, u32[]{:S(2)}) copy-start(f32[64]{0:T(128)} %param.10) | copy-start | bytes 772
  0.0 81.3 %copy-start = (bf16[64,1024]{1,0:T(8,128)(2,1)S(1)}, bf16[64,1024]{1,0:T(8,128)(2,1)}, u32[]{:S(2)}) copy-start(bf16[64,1024]{1,0:T(8,128)(2,1)} %param.9) | copy-start | bytes 393220

commit v3 on v2

--- a/solution.py
+++ b/solution.py
@@ -22,7 +22,7 @@
 SLOT = {unit: slot for slot, unit in enumerate(UNITS)}
 GROUPS = ((0, 1), (1, 3), (3, 6), (6, 11), (11, 15), (15, 16))
 GROUP_AT = (3.5, 6.5, 10.5, 15.5, 19.0, 21.5)
-HOP = 3.5
+HOP = 20.0
 DYS = (0, 1, -1, 2)
 
 

time: 83.3 us -> 75.3 us (0.904)
  the two profiles are of different devices: /device:TPU:60 before, /device:TPU:18 now
where the time goes in v3:
time: 75.3 us; the launch traced here: 75.1 us
  Pallas kernels  71.9 us (95%)
  other arithmetic  1.76 us (2%)
  local copies, waits for them, and re-layouts  1.4 us (2%)
    pallas_call x1, Pallas kernels, gathered_product(): pl.pallas_call(kernel, out_shape=jax.ShapeDtypeStruct((rows, width), jnp....  71.9 us
    div x1, other arithmetic, shards(): return (driving.astype(jnp.float32) + ladder) / denom  1.76 us

profile of v3, /device:TPU:18, one launch (start us, length us, event | category | flops | bytes accessed | tf_op | source)
XLA Modules:
  0.0 75.1 jit_solution(17885362378558485043)
XLA Ops:
  0.0 0.0 copy-start.1
  0.0 0.0 copy-start.2
  0.0 0.0 copy-start
  0.0 1.4 %copy.7.mask_ref = s32[16,8]{1,0:T(8,128)} copy(s32[16,8]{0,1:T(8,128)} %param.8) | data formatting | bytes 1024 | tf_op args[2]
  1.4 71.9 %ladder.1 = f32[64,1024]{1,0:T(8,128)} custom-call(bf16[32,2048]{1,0:T(8,128)(2,1)} %a_ref.1, bf16[2048,1024]{1,0:T(8,128)(2,1)} %m_hbm.1, s32[16,8]{1,0:T(8,128)} %copy.7.mask_ref), custom_call_target="tpu_custom_call" | custom-call | tf_op jit(solution)/shard_map/ladder/pallas_call | solution.py:364
  73.3 0.0 copy-done.1
  73.3 0.0 copy-done.2
  73.3 0.0 copy-done
  73.4 1.8 %subtract_divide_fusion = f32[64,1024]{1,0:T(8,128)} fusion(f32[64,1024]{1,0:T(8,128)} %ladder.1, bf16[64,1024]{1,0:T(8,128)(2,1)S(1)} %copy-done, f32[64]{0:T(128)S(1)} %copy-done.2, f32[1024]{0:T(1024)S(1)} %copy-done.1), kind=kLoop, calls=%fused_computation | loop fusion | flops 262144 | bytes 659712 | tf_op jit(solution)/shard_map/div | solution.py:405
Async XLA Ops:
  0.0 73.3 %copy-start.1 = (f32[1024]{0:T(1024)S(1)}, f32[1024]{0:T(1024)}, u32[]{:S(2)}) copy-start(f32[1024]{0:T(1024)} %param.11) | copy-start | bytes 12292
  0.0 73.3 %copy-start.2 = (f32[64]{0:T(128)S(1)}, f32[64]{0:T(128)}, u32[]{:S(2)}) copy-start(f32[64]{0:T(128)} %param.10) | copy-start | bytes 772
  0.0 73.3 %copy-start = (bf16[64,1024]{1,0:T(8,128)(2,1)S(1)}, bf16[64,1024]{1,0:T(8,128)(2,1)}, u32[]{:S(2)}) copy-start(bf16[64,1024]{1,0:T(8,128)(2,1)} %param.9) | copy-start | bytes 393220

commit v4 on v3

--- a/solution.py
+++ b/solution.py
@@ -265,7 +265,7 @@
                 device_id=mate, device_id_type=MESH),
         )
 
-    def act_end(slot):
+    def act_end(slot, give):
         def run():
             d, p, down, first, lo = where_is(slot)
 
@@ -276,19 +276,16 @@
                 return (own_part(slot, t) + decode(q_in.at[slot, 0], s_in.at[slot, 0], t)
                         + decode(q_in.at[slot, 1], s_in.at[slot, 1], t))
 
-            @pl.when((d == 0) & (lo != y_lo))
+            @pl.when((d == 0) & ((lo != y_lo) if give else (lo == y_lo)))
             def _():
                 def go(t):
-                    encode(summed(t), yq_out, ys_out, t)
-                    for copy in y_copies(t):
-                        copy.start()
+                    if give:
+                        encode(summed(t), yq_out, ys_out, t)
+                        for copy in y_copies(t):
+                            copy.start()
+                    else:
+                        total[:, pl.ds(pl.multiple_of(t * lanes, lanes), lanes)] = summed(t)
                 over_lanes(go)
-
-            @pl.when((d == 0) & (lo == y_lo))
-            def _():
-                def keep(t):
-                    total[:, pl.ds(pl.multiple_of(t * lanes, lanes), lanes)] = summed(t)
-                over_lanes(keep)
         return run
 
     acts = []
@@ -315,7 +312,8 @@
             acts.append((at + 0.01, act_start(slot)))
             for k in (3, 2, 1):
                 acts.append((at + 1.0 + HOP * (4 - k), act_hop(slot, k)))
-            acts.append((at + 1.0 + HOP * 4, act_end(slot)))
+            acts.append((at + 1.0 + HOP * 4, act_end(slot, True)))
+            acts.append((at + 1.0 + HOP * 6, act_end(slot, False)))
     acts.sort(key=lambda act: act[0])
 
     sibling_kinds = []

time: 75.3 us -> 75.3 us (level)
  no operation moved by 1% of the time
where the time goes in v4:
time: 75.3 us; the launch traced here: 75.1 us
  Pallas kernels  71.9 us (95%)
  other arithmetic  1.76 us (2%)
  local copies, waits for them, and re-layouts  1.4 us (2%)
    pallas_call x1, Pallas kernels, gathered_product(): pl.pallas_call(kernel, out_shape=jax.ShapeDtypeStruct((rows, width), jnp....  71.9 us
    div x1, other arithmetic, shards(): return (driving.astype(jnp.float32) + ladder) / denom  1.76 us

profile of v4, /device:TPU:18, one launch (start us, length us, event | category | flops | bytes accessed | tf_op | source)
XLA Modules:
  0.0 75.1 jit_solution(2268552374245878381)
XLA Ops:
  0.0 0.0 copy-start.1
  0.0 0.0 copy-start.2
  0.0 0.0 copy-start
  0.0 1.4 %copy.7.mask_ref = s32[16,8]{1,0:T(8,128)} copy(s32[16,8]{0,1:T(8,128)} %param.8) | data formatting | bytes 1024 | tf_op args[2]
  1.4 71.9 %ladder.1 = f32[64,1024]{1,0:T(8,128)} custom-call(bf16[32,2048]{1,0:T(8,128)(2,1)} %a_ref.1, bf16[2048,1024]{1,0:T(8,128)(2,1)} %m_hbm.1, s32[16,8]{1,0:T(8,128)} %copy.7.mask_ref), custom_call_target="tpu_custom_call" | custom-call | tf_op jit(solution)/shard_map/ladder/pallas_call | solution.py:362
  73.3 0.0 copy-done.1
  73.3 0.0 copy-done.2
  73.4 0.0 copy-done
  73.4 1.8 %subtract_divide_fusion = f32[64,1024]{1,0:T(8,128)} fusion(f32[64,1024]{1,0:T(8,128)} %ladder.1, bf16[64,1024]{1,0:T(8,128)(2,1)S(1)} %copy-done, f32[64]{0:T(128)S(1)} %copy-done.2, f32[1024]{0:T(1024)S(1)} %copy-done.1), kind=kLoop, calls=%fused_computation | loop fusion | flops 262144 | bytes 659712 | tf_op jit(solution)/shard_map/div | solution.py:403
Async XLA Ops:
  0.0 73.3 %copy-start.1 = (f32[1024]{0:T(1024)S(1)}, f32[1024]{0:T(1024)}, u32[]{:S(2)}) copy-start(f32[1024]{0:T(1024)} %param.11) | copy-start | bytes 12292
  0.0 73.3 %copy-start.2 = (f32[64]{0:T(128)S(1)}, f32[64]{0:T(128)}, u32[]{:S(2)}) copy-start(f32[64]{0:T(128)} %param.10) | copy-start | bytes 772
  0.0 73.4 %copy-start = (bf16[64,1024]{1,0:T(8,128)(2,1)S(1)}, bf16[64,1024]{1,0:T(8,128)(2,1)}, u32[]{:S(2)}) copy-start(bf16[64,1024]{1,0:T(8,128)(2,1)} %param.9) | copy-start | bytes 393220
